TPU v7x, 32 devices: a whole 2x2x4 slice. The times are simulated.
32 devices in a mesh: row: 8 (over z, x), col: 4 (over y, core).
Axes of the slice: x: 2, y: 2, z: 4, core: 2. Of those that a mesh axis runs over, the one named last changes fastest.
Arguments:
- hidden: bfloat16 [4, 20480, 768], P(None, ('row', 'col')), may hold values from -6 to 6
- grad_out: bfloat16 [4, 20480, 1024], P(None, ('row', 'col')), may hold values from -6 to 6
- counts: int32 [32, 4], P(('row', 'col')), may hold values from 1 to 640, as said below
- shadow_ids: int32 [4], replicated, may hold values from 0 to 59, as said below
- master: float32 [60, 768, 1024], P(None, 'row', 'col'), may hold values from -0.21875 to 0.21875
- momentum: float32 [60, 768, 1024], P(None, 'row', 'col'), may hold values from -6 to 6
Outputs:
- master_out: float32 [60, 768, 1024], P(None, 'row', 'col')
- momentum_out: float32 [60, 768, 1024], P(None, 'row', 'col')
- shadow_out: bfloat16 [4, 768, 1024], P(None, 'row')
Inputs may be any that keep to these rules, and one draw needn't show every extreme that they name: counts are at most 640, and some device reaches 640 for some shadowed expert. `shadow_ids`: the 4 ids are distinct, and experts 0 and 59 are always among them.
All inputs are finite; a program needn't handle non-finite values.
Results may differ from a plain program's by a relative error of at most 0.007.
Values may be sent and summed in bfloat16 or wider, within the bound.
A program may use at most 128 MiB of HBM per device.

v0:
```python
import jax
import jax.numpy as jnp
from jax import lax
from jax.sharding import PartitionSpec as P

momentum_decay = 0.9
step_size = 0.01


def dense_gradient(hidden, grad_out, live_counts):
    positions = jnp.arange(hidden.shape[1], dtype=jnp.int32)
    live_mask = positions[None, :] < live_counts[:, None]
    masked = jnp.where(live_mask[:, :, None], hidden, jnp.zeros((), jnp.bfloat16))
    return jnp.einsum("etf,etd->efd", masked, grad_out, preferred_element_type=jnp.float32)


def shards(hidden, grad_out, counts, shadow_ids, master, momentum):
    live_counts = counts[0]
    gradient = dense_gradient(hidden, grad_out, live_counts)
    summed = lax.psum_scatter(
        gradient.astype(jnp.bfloat16), "row", scatter_dimension=1, tiled=True
    ).astype(jnp.float32)
    summed = lax.psum_scatter(
        summed.astype(jnp.bfloat16), "col", scatter_dimension=2, tiled=True
    ).astype(jnp.float32)
    devices = lax.axis_size("row") * lax.axis_size("col")
    summed = summed * jnp.float32((hidden.shape[1] * devices) ** (-0.5))
    new_momentum = momentum_decay * momentum[shadow_ids] + summed
    new_master = master[shadow_ids] - step_size * new_momentum
    momentum_out = momentum.at[shadow_ids].set(new_momentum)
    master_out = master.at[shadow_ids].set(new_master)
    shadow_out = lax.all_gather(new_master.astype(jnp.bfloat16), "col", axis=2, tiled=True)
    return (master_out, momentum_out, shadow_out)


def solution(mesh):
    return jax.shard_map(
        shards,
        mesh=mesh,
        in_specs=(
            P(None, ("row", "col"), None),
            P(None, ("row", "col"), None),
            P(("row", "col"), None),
            P(),
            P(None, "row", "col"),
            P(None, "row", "col"),
        ),
        out_specs=(P(None, "row", "col"), P(None, "row", "col"), P(None, "row", None)),
        check_vma=False,
    )
```

profile of v0, /device:TPU:0, one launch (start us, length us, event | category | flops | bytes accessed | tf_op | source)
XLA Modules:
  0.0 193.6 jit_solution(1493444020295759507)
XLA Ops:
  7.2 0.0 reduce-scatter.3.cloned.1.call-start
  7.2 0.0 copy-start
  7.2 0.0 slice-start
  7.2 6.5 %copy.16 = f32[60,96,256]{2,1,0:T(8,128)} copy(f32[60,96,256]{2,1,0:T(8,128)} %param.10) | data formatting | bytes 11796480
  13.7 0.0 copy-done
  13.7 0.0 copy-start.1
  13.7 0.0 slice-start.1
  13.7 0.0 copy-start.2
  13.8 3.0 %copy.17 = f32[60,96,256]{2,1,0:T(8,128)} copy(f32[60,96,256]{2,1,0:T(8,128)S(1)} %copy-done) | data formatting | bytes 11796480
  16.7 0.0 copy-done.1
  16.8 0.1 iota_compare_fusion
  16.8 0.0 slice-done
  16.8 0.0 slice-done.1
  16.8 1.9 %copy-done.2 = bf16[4,640,768]{2,1,0:T(8,128)(2,1)S(1)} copy-done((bf16[4,640,768]{2,1,0:T(8,128)(2,1)S(1)}, bf16[4,640,768]{2,1,0:T(8,128)(2,1)}, u32[]{:S(2)}) %copy-start.2) | copy-done | bytes 3932184
  18.8 7.4 %fusion.3 = bf16[4,768,1024]{2,1,0:T(8,128)(2,1)} fusion(bf16[4,640,1024]{2,1,0:T(8,128)(2,1)S(1)} %bitcast.4, bf16[4,640,768]{2,1,0:T(8,128)(2,1)S(1)} %copy-done.2, pred[4,640]{1,0:T(4,128)(4,1)S(1)} %iota_compare_fusion), kind=kOutput, calls=%fused_computation.7 | convolution fusion | flops 4031643648 | bytes 15469056 | tf_op jit(solution)/shard_map/etf,etd->efd/dot_general | solution.py:14
  26.1 0.0 copy-start.3
  26.1 0.0 reduce-scatter.3.cloned.1.call-update
  26.2 0.0 reduce-scatter.5.cloned.1.call-start
  26.2 120.9 %reduce-scatter.3.cloned.1.call-done = bf16[4,96,1024]{2,1,0:T(8,128)(2,1)} async-done(((bf16[4,768,1024]{2,1,0:T(8,128)(2,1)}), bf16[4,96,1024]{2,1,0:T(8,128)(2,1)}) %reduce-scatter.3.cloned.1.call-update) | async-done | bytes 786448 | tf_op jit(solution)/shard_map/reduce_scatter | solution.py:20
  147.1 0.0 reduce-scatter.5.cloned.1.call-update
  147.1 0.0 copy-done.3
  147.2 3.2 %gather_fusion = f32[4,96,256]{2,1,0:T(8,128)S(1)} fusion(f32[60,96,256]{2,1,0:T(8,128)} %copy.16, s32[1024]{0:T(1024)S(1)} %pad_clamp_fusion), kind=kCustom, calls=%fused_computation | custom fusion | bytes 786448 | tf_op jit(solution)/shard_map/gather | solution.py:29
  150.4 3.2 %gather_fusion.1 = f32[4,96,256]{2,1,0:T(8,128)S(1)} fusion(f32[60,96,256]{2,1,0:T(8,128)} %copy.17, s32[1024]{0:T(1024)S(1)} %pad_clamp_fusion), kind=kCustom, calls=%fused_computation.1 | custom fusion | bytes 786448 | tf_op jit(solution)/shard_map/gather | solution.py:28
  153.7 18.5 %reduce-scatter.5.cloned.1.call-done = bf16[4,96,256]{2,1,0:T(8,128)(2,1)} async-done(((bf16[4,96,1024]{2,1,0:T(8,128)(2,1)}), bf16[4,96,256]{2,1,0:T(8,128)(2,1)}) %reduce-scatter.5.cloned.1.call-update) | async-done | bytes 196624 | tf_op jit(solution)/shard_map/reduce_scatter | solution.py:23
  172.1 1.0 fusion.8
  173.2 2.3 %scatter_fusion = f32[60,96,256]{2,1,0:T(8,128)} fusion(f32[60,96,256]{2,1,0:T(8,128)} %copy.16, s32[4]{0:T(128)S(1)} %compare_select_fusion, f32[4,96,256]{2,1,0:T(8,128)S(1)} %get-tuple-element.4), kind=kCustom, calls=%fused_computation.2 | custom fusion | bytes 1179664 | tf_op jit(solution)/shard_map/scatter | solution.py:31
  175.5 2.3 %scatter_fusion.1 = f32[60,96,256]{2,1,0:T(8,128)} fusion(f32[60,96,256]{2,1,0:T(8,128)} %copy.17, s32[4]{0:T(128)S(1)} %compare_select_fusion, f32[4,96,256]{2,1,0:T(8,128)S(1)} %get-tuple-element.5), kind=kCustom, calls=%fused_computation.3 | custom fusion | bytes 1179664 | tf_op jit(solution)/shard_map/scatter | solution.py:30
  177.9 8.0 %all_gather.3 = bf16[4,96,1024]{2,1,0:T(8,128)(2,1)S(1)} all-gather(bf16[4,96,256]{2,1,0:T(8,128)(2,1)S(1)} %get-tuple-element.3), channel_id=1, replica_groups=mesh['row'=8,'col'=4] {'col'}, dimensions={2}, use_global_device_ids=true | all-gather | bytes 983040 | tf_op jit(solution)/shard_map/all_gather | solution.py:32
  185.9 0.9 copy.18
  (3 shorter events, 0.0 us)
Async XLA Ops:
  7.2 139.9 %reduce-scatter.3.cloned.1.call-start = ((), (), s32[]{:S(2)}) async-start(), calls=%async_computation.2 | async-start | bytes 7077888 | tf_op jit(solution)/shard_map/reduce_scatter | solution.py:20
  7.2 6.5 %copy-start = (f32[60,96,256]{2,1,0:T(8,128)S(1)}, f32[60,96,256]{2,1,0:T(8,128)}, u32[]{:S(2)}) copy-start(f32[60,96,256]{2,1,0:T(8,128)} %param.11) | copy-start | bytes 17694724
  7.2 9.6 %slice-start = ((s8[5242880]{0:T(1024)(128)(4,1)}), s8[4194304]{0:T(1024)(128)(4,1)S(1)}, s32[]{:S(2)}) async-start(s8[5242880]{0:T(1024)(128)(4,1)} %bitcast.3), calls=%async_computation.4 | async-start | bytes 8388608
  13.7 3.0 %copy-start.1 = (s32[1,4]{1,0:T(1,128)S(1)}, s32[1,4]{1,0:T(1,128)}, u32[]{:S(2)}) copy-start(s32[1,4]{1,0:T(1,128)} %param.8) | copy-start | bytes 52
  13.7 3.1 %slice-start.1 = ((s8[5242880]{0:T(1024)(128)(4,1)}), s8[1048576]{0:T(1024)(128)(4,1)S(1)}, s32[]{:S(2)}) async-start(s8[5242880]{0:T(1024)(128)(4,1)} %bitcast.3), calls=%async_computation.5 | async-start | bytes 2097152
  13.7 5.0 %copy-start.2 = (bf16[4,640,768]{2,1,0:T(8,128)(2,1)S(1)}, bf16[4,640,768]{2,1,0:T(8,128)(2,1)}, u32[]{:S(2)}) copy-start(bf16[4,640,768]{2,1,0:T(8,128)(2,1)} %param.6) | copy-start | bytes 11796484
  26.1 121.0 %copy-start.3 = (s32[4]{0:T(128)S(1)}, s32[4]{0:T(128)}, u32[]{:S(2)}) copy-start(s32[4]{0:T(128)} %param.9) | copy-start | bytes 52
  26.2 146.0 %reduce-scatter.5.cloned.1.call-start = ((), (), s32[]{:S(2)}) async-start(), calls=%async_computation.3 | async-start | bytes 983040 | tf_op jit(solution)/shard_map/reduce_scatter | solution.py:23
Sparse Core Ops, SparseCore 0:
  26.3 120.7 reduce-scatter.2
  149.6 22.4 reduce-scatter.4
where the time goes:
time: 194 us
  waiting for transfers between devices  139 us (72%)
  local copies, waits for them, and re-layouts  23.5 us (12%)
  between operations  14.1 us (7%)
  blocking collectives  8 us (4%)
  matrix products  7.35 us (4%)
    reduce_scatter x1, waiting for transfers between devices, shards(): lax.psum_scatter(gradient.astype(jnp.bfloat16), 'row', scatter_dimension=...  121 us
    reduce_scatter x1, waiting for transfers between devices, shards(): lax.psum_scatter(summed.astype(jnp.bfloat16), 'col', scatter_dimension=2,...  18.5 us
    unnamed x15, local copies, waits for them, and re-layouts  12.3 us
    all_gather x1, blocking collectives, shards(): lax.all_gather(new_master.astype(jnp.bfloat16), 'col', axis=2, tiled=True)  8 us
    dot_general x1, matrix products, dense_gradient(): jnp.einsum('etf,etd->efd', masked, grad_out, preferred_element_type=jnp.f...  7.35 us
  transfers between devices with their start and end apart: 2, of which 2 were waited for; matrix products, arithmetic and copies ran while one was open for 3% of the time, Pallas kernels for 0%

commit v1 on v0

v1 whole, which is shorter than its diff:
```python
import functools

import jax
import jax.numpy as jnp
from jax import lax
from jax.experimental import pallas as pl
from jax.experimental.pallas import tpu as pltpu
from jax.sharding import PartitionSpec as P

momentum_decay = 0.9
step_size = 0.01
bf16, f32 = jnp.bfloat16, jnp.float32
MESH = pl.DeviceIdType.MESH


def gather_body(ids, w_ref, m_ref, w_out, m_out):
    w_out[...] = w_ref[...]
    m_out[...] = m_ref[...]


def scatter_body(ids, w_new, m_new, w_any, m_any, w_out, m_out):
    w_out[...] = w_new[...]
    m_out[...] = m_new[...]


def reduce_body(sizes, counts, hidden, grad, w_rows, m_rows, w_new, m_new, shadow,
                h_in, g_in, h_t, part, r_core, s_core, rx1, sx1, rx2, ry1, sy1, ry2, s_last, r_last,
                in_sem, core_sem, one_sem, two_sem, last_sem, ag_sem, fw_sem):
    experts, cap, outer_row, outer_col, feat, width, halves, scale = sizes
    chunks = experts * halves
    row, col = lax.axis_index("row"), lax.axis_index("col")
    z, x = row // 2, row % 2
    y, core = col // 2, col % 2

    def spots(name):
        if name == "core":
            return [(1 - core, (row, y * 2 + 1 - core))]
        if name == "x":
            return [(1 - x, (z * 2 + 1 - x, col))]
        if name == "y":
            others = [lax.rem(y + d, outer_col) for d in range(1, outer_col)]
            return [(t, (row, t * 2 + core)) for t in others]
        others = [lax.rem(z + d, outer_row) for d in range(1, outer_row)]
        return [(t, (t * 2 + x, col)) for t in others]

    loads = []
    for e in range(experts):
        pair = (
            pltpu.make_async_copy(hidden.at[e], h_in.at[e], in_sem.at[0, e]),
            pltpu.make_async_copy(grad.at[e], g_in.at[e], in_sem.at[1, e]),
        )
        for copy in pair:
            copy.start()
        loads.append(pair)

    barrier = pltpu.get_barrier_semaphore()
    greeted = [where for name in ("core", "x", "y", "z") for _, where in spots(name)]
    for where in greeted:
        pl.semaphore_signal(barrier, inc=1, device_id=where, device_id_type=MESH)

    started = []

    def send(src, dst, sem, where):
        copy = pltpu.make_async_remote_copy(
            src_ref=src, dst_ref=dst, send_sem=sem.at[0], recv_sem=sem.at[1],
            device_id=where, device_id_type=MESH,
        )
        copy.start()
        started.append(copy)
        return copy

    flight = {}

    def multiply(e):
        for copy in loads[e]:
            copy.wait()
        live = lax.broadcasted_iota(jnp.int32, (cap, h_in.shape[2]), 0) < counts[0, e]
        h_t[...] = jnp.where(live, h_in[e], jnp.zeros((), bf16)).T
        block = halves * width
        step = max(256, block)
        for first in range(0, g_in.shape[2], step):
            got = jnp.dot(h_t[...], g_in[e, :, first:first + step], preferred_element_type=f32).astype(bf16)
            for k in range(step // block):
                at = first // block + k
                for h in range(halves):
                    cut = got[:, k * block + h * width:k * block + (h + 1) * width]
                    part[e * halves + h, at // 2, at % 2] = cut.reshape(outer_row, 2, feat, width)
        if e == 0:
            pl.semaphore_wait(barrier, len(greeted))
        for h in range(halves):
            c = e * halves + h
            ((t, where),) = spots("core")
            flight["core", c] = [send(part.at[c, :, t], r_core.at[c], core_sem.at[c], where)]

    def first(c):
        for copy in flight["core", c]:
            copy.wait_recv()
        for b in range(outer_col):
            s_core[c, b] = (part[c, b, core].astype(f32) + r_core[c, b].astype(f32)).astype(bf16)
        i = c // 2
        if c % 2 == 0:
            ((t, where),) = spots("x")
            flight["one", c] = [send(s_core.at[c, :, :, t], rx1.at[i], one_sem.at[c, 0], where)]
        else:
            flight["one", c] = [
                send(s_core.at[c, t], ry1.at[i, d], one_sem.at[c, d], where)
                for d, (t, where) in enumerate(spots("y"))
            ]

    def second(c):
        for copy in flight["one", c]:
            copy.wait_recv()
        i = c // 2
        if c % 2 == 0:
            for b in range(outer_col):
                sx1[i, b] = (s_core[c, b, :, x].astype(f32) + rx1[i, b].astype(f32)).astype(bf16)
            flight["two", c] = [
                send(sx1.at[i, t], rx2.at[i, d], two_sem.at[c, d], where)
                for d, (t, where) in enumerate(spots("y"))
            ]
        else:
            total = s_core[c, y].astype(f32)
            for d in range(outer_col - 1):
                total = total + ry1[i, d].astype(f32)
            sy1[i] = total.astype(bf16)
            ((t, where),) = spots("x")
            flight["two", c] = [send(sy1.at[i, :, t], ry2.at[i], two_sem.at[c, 0], where)]

    def third(c):
        for copy in flight["two", c]:
            copy.wait_recv()
        i = c // 2
        if c % 2 == 0:
            total = sx1[i, y].astype(f32)
            for d in range(outer_col - 1):
                total = total + rx2[i, d].astype(f32)
        else:
            total = sy1[i, :, x].astype(f32) + ry2[i].astype(f32)
        s_last[c] = total.astype(bf16)
        flight["last", c] = [
            send(s_last.at[c, t], r_last.at[c, d], last_sem.at[c, d], where)
            for d, (t, where) in enumerate(spots("z"))
        ]

    def fourth(c):
        for copy in flight["last", c]:
            copy.wait_recv()
        total = s_last[c, z].astype(f32)
        for d in range(outer_row - 1):
            total = total + r_last[c, d].astype(f32)
        e, lanes = c // halves, slice(c % halves * width, (c % halves + 1) * width)
        moved = momentum_decay * m_rows[e, :, lanes] + total * f32(scale)
        m_new[e, :, lanes] = moved
        stepped = w_rows[e, :, lanes] - step_size * moved
        w_new[e, :, lanes] = stepped
        shadow[y, core, c] = stepped.astype(bf16)
        own = shadow.at[y, core, c]
        flight["ag", c] = [
            send(own, own, ag_sem.at[c, d], where) for d, (t, where) in enumerate(spots("y"))
        ]

    def fifth(c):
        for copy in flight["ag", c]:
            copy.wait_recv()
        ((t, where),) = spots("core")
        ours = shadow.at[:, core, c]
        flight["fw", c] = [send(ours, ours, fw_sem.at[c], where)]

    stages = (first, second, third, fourth, fifth)
    plan = [("m", 0), ("m", 1), (0, 0), ("m", 2), (0, 1)]
    plan += [("m", e) for e in range(3, experts)]
    for tick in range(experts + 4):
        for stage, e in ((1, tick), (2, tick - 1), (0, tick + 2), (3, tick - 2), (4, tick - 3)):
            if 0 <= e < experts:
                plan.append((stage, e))
    for stage, e in plan:
        if stage == "m":
            multiply(e)
            continue
        for h in range(halves):
            stages[stage](e * halves + h)
    for c in range(chunks):
        for copy in flight["fw", c]:
            copy.wait_recv()
    for copy in started:
        copy.wait_send()


def shards(hidden, grad_out, counts, shadow_ids, master, momentum):
    experts, cap, hid = hidden.shape
    out = grad_out.shape[2]
    n_row, n_col = lax.axis_size("row"), lax.axis_size("col")
    feat, block = master.shape[1:]
    halves = 2 if block % 256 == 0 else 1
    width = block // halves
    chunks = experts * halves
    outer_row, outer_col = n_row // 2, n_col // 2
    scale = (cap * n_row * n_col) ** (-0.5)
    pairs = (chunks + 1) // 2

    row_of = pl.BlockSpec((1, feat, block), lambda i, ids: (ids[i], 0, 0))
    row_at = pl.BlockSpec((1, feat, block), lambda i, ids: (i, 0, 0))
    rows_type = jax.ShapeDtypeStruct((experts, feat, block), f32)
    w_rows, m_rows = pl.pallas_call(
        gather_body,
        grid_spec=pltpu.PrefetchScalarGridSpec(
            num_scalar_prefetch=1, grid=(experts,), in_specs=[row_of, row_of], out_specs=[row_at, row_at]
        ),
        out_shape=[rows_type, rows_type],
        name="pick_rows",
    )(shadow_ids, master, momentum)

    sizes = (experts, cap, outer_row, outer_col, feat, width, halves, scale)
    tail = (feat, width)
    oc1, or1 = max(outer_col - 1, 1), max(outer_row - 1, 1)
    vmem = pl.BlockSpec(memory_space=pltpu.VMEM)
    anywhere = pl.BlockSpec(memory_space=pl.ANY)
    dma = pltpu.SemaphoreType.DMA
    w_new, m_new, shadow = pl.pallas_call(
        functools.partial(reduce_body, sizes),
        in_specs=[pl.BlockSpec(memory_space=pltpu.SMEM), anywhere, anywhere, vmem, vmem],
        out_specs=[vmem, vmem, vmem],
        out_shape=[rows_type, rows_type, jax.ShapeDtypeStruct((outer_col, 2, chunks) + tail, bf16)],
        scratch_shapes=[
            pltpu.VMEM((experts, cap, hid), bf16),
            pltpu.VMEM((experts, cap, out), bf16),
            pltpu.VMEM((hid, cap), bf16),
            pltpu.VMEM((chunks, outer_col, 2, outer_row, 2) + tail, bf16),
            pltpu.VMEM((chunks, outer_col, outer_row, 2) + tail, bf16),
            pltpu.VMEM((chunks, outer_col, outer_row, 2) + tail, bf16),
            pltpu.VMEM((pairs, outer_col, outer_row) + tail, bf16),
            pltpu.VMEM((pairs, outer_col, outer_row) + tail, bf16),
            pltpu.VMEM((pairs, oc1, outer_row) + tail, bf16),
            pltpu.VMEM((pairs, oc1, outer_row, 2) + tail, bf16),
            pltpu.VMEM((pairs, outer_row, 2) + tail, bf16),
            pltpu.VMEM((pairs, outer_row) + tail, bf16),
            pltpu.VMEM((chunks, outer_row) + tail, bf16),
            pltpu.VMEM((chunks, or1) + tail, bf16),
            dma((2, experts)),
            dma((chunks, 2)),
            dma((chunks, oc1, 2)),
            dma((chunks, oc1, 2)),
            dma((chunks, or1, 2)),
            dma((chunks, oc1, 2)),
            dma((chunks, 2)),
        ],
        compiler_params=pltpu.CompilerParams(
            collective_id=0, has_side_effects=True, vmem_limit_bytes=60 * 1024 * 1024
        ),
        cost_estimate=pl.CostEstimate(
            flops=2 * experts * cap * hid * out, bytes_accessed=2 * experts * cap * (hid + out), transcendentals=0
        ),
        name="reduce_step",
    )(counts, hidden, grad_out, w_rows, m_rows)

    master_out, momentum_out = pl.pallas_call(
        scatter_body,
        grid_spec=pltpu.PrefetchScalarGridSpec(
            num_scalar_prefetch=1, grid=(experts,),
            in_specs=[row_at, row_at, anywhere, anywhere], out_specs=[row_of, row_of],
        ),
        out_shape=[jax.ShapeDtypeStruct(master.shape, f32)] * 2,
        input_output_aliases={3: 0, 4: 1},
        name="put_rows",
    )(shadow_ids, w_new, m_new, master, momentum)
    shadow = shadow.reshape(n_col, experts, halves, feat, width)
    shadow_out = shadow.transpose(1, 3, 0, 2, 4).reshape(experts, feat, out)
    return (master_out, momentum_out, shadow_out)


def solution(mesh):
    return jax.shard_map(
        shards,
        mesh=mesh,
        in_specs=(
            P(None, ("row", "col"), None),
            P(None, ("row", "col"), None),
            P(("row", "col"), None),
            P(),
            P(None, "row", "col"),
            P(None, "row", "col"),
        ),
        out_specs=(P(None, "row", "col"), P(None, "row", "col"), P(None, "row", None)),
        check_vma=False,
    )
```

time: 194 us -> 70.7 us (0.36)
  waiting for transfers between devices: 139 us -> 0 us
  Pallas kernels: 0 us -> 58.9 us
  between operations: 14.1 us -> 0.66 us
  local copies, waits for them, and re-layouts: 23.5 us -> 10.7 us
  blocking collectives: 8 us -> 0 us
  matrix products: 7.35 us -> 0 us
    reduce_scatter x2 -> x0, waiting for transfers between devices: 139 us -> none  [the longest x1 121 us: shards(): lax.psum_scatter(gradient.astype(jnp.bfloat16), 'row', scatter_dimension=...]
    pallas_call x0 -> x3, Pallas kernels: none -> 58.9 us  [the longest x1 50.9 us: shards(): pl.pallas_call(functools.partial(reduce_body, sizes), in_specs=[pl.BlockS...]
    all_gather x1 -> x0, blocking collectives: 8 us -> none  [shards(): lax.all_gather(new_master.astype(jnp.bfloat16), 'col', axis=2, tiled=True)]
    dot_general x1 -> x0, matrix products: 7.35 us -> none  [dense_gradient(): jnp.einsum('etf,etd->efd', masked, grad_out, preferred_element_type=jnp.f...]
    gather x2 -> x0, local copies, waits for them, and re-layouts: 6.49 us -> none  [the longest x1 3.25 us: shards(): new_master = master[shadow_ids] - step_size * new_momentum]
    scatter x2 -> x0, local copies, waits for them, and re-layouts: 4.69 us -> none  [the longest x1 2.35 us: shards(): master_out = master.at[shadow_ids].set(new_master)]
    unnamed x15 -> x6, local copies, waits for them, and re-layouts: 12.3 us -> 8.66 us
  transfers between devices with their start and end apart: 2 -> 0, of which waited for: 2 -> 0; matrix products, arithmetic and copies ran while one was open for 3% -> 0% of each run, Pallas kernels for 0% -> 0%
where the time goes in v1:
time: 70.7 us; the launch traced here: 70.3 us
  Pallas kernels  58.9 us (83%)
  local copies, waits for them, and re-layouts  10.7 us (15%)
    pallas_call x1, Pallas kernels, shards(): pl.pallas_call(functools.partial(reduce_body, sizes), in_specs=[pl.BlockS...  50.9 us
    unnamed x6, local copies, waits for them, and re-layouts  8.66 us
    pallas_call x1, Pallas kernels, shards(): pl.pallas_call(scatter_body, grid_spec=pltpu.PrefetchScalarGridSpec(num_s...  4.1 us
    pallas_call x1, Pallas kernels, shards(): pl.pallas_call(gather_body, grid_spec=pltpu.PrefetchScalarGridSpec(num_sc...  3.95 us
    reshape x1, local copies, waits for them, and re-layouts, shards(): shadow_out = shadow.transpose(1, 3, 0, 2, 4).reshape(experts, feat, out)  1.44 us

profile of v1, /device:TPU:0, one launch (start us, length us, event | category | flops | bytes accessed | tf_op | source)
XLA Modules:
  0.0 70.3 jit_solution(13494001473025998310)
XLA Ops:
  0.6 0.0 copy-start
  0.6 6.1 %copy.17.m_ref.m_any = f32[60,96,256]{2,1,0:T(8,128)} copy(f32[60,96,256]{2,1,0:T(8,128)} %param.11) | data formatting | bytes 11796480
  6.7 0.0 copy-done
  6.7 2.6 %copy.16.w_ref.w_any = f32[60,96,256]{2,1,0:T(8,128)} copy(f32[60,96,256]{2,1,0:T(8,128)S(1)} %copy-done) | data formatting | bytes 11796480
  9.3 3.9 %pick_rows.1 = (f32[4,96,256]{2,1,0:T(8,128)}, f32[4,96,256]{2,1,0:T(8,128)}) custom-call(s32[4]{0:T(128)} %ids.3, f32[60,96,256]{2,1,0:T(8,128)} %copy.16.w_ref.w_any, f32[60,96,256]{2,1,0:T(8,128)} %copy.17.m_ref.m_any), custom_call_target="tpu_custom_call" | custom-call | tf_op jit(solution)/shard_map/pick_rows/pallas_call | solution.py:204
  13.2 50.9 %reduce_step.1 = (f32[4,96,256]{2,1,0:T(8,128)}, f32[4,96,256]{2,1,0:T(8,128)}, bf16[2,2,8,96,128]{4,3,2,1,0:T(8,128)(2,1)}) custom-call(s32[1,4]{1,0:T(1,128)} %counts.1, bf16[4,640,768]{2,1,0:T(8,128)(2,1)} %hidden.1, bf16[4,640,1024]{2,1,0:T(8,128)(2,1)} %grad.1, f32[4,96,256]{2,1,0:T(8,128)} %get-tuple-element.10.w_rows, ...), custom_call_target="tpu_custom_call" | custom-call | flops 4026531840 | bytes 9175040 | tf_op jit(solution)/shard_map/reduce_step/pallas_call | solution.py:219
  64.2 0.0 copy-start.1
  64.2 4.1 %put_rows.1 = (f32[60,96,256]{2,1,0:T(8,128)}, f32[60,96,256]{2,1,0:T(8,128)}) custom-call(s32[4]{0:T(128)} %ids.3, f32[4,96,256]{2,1,0:T(8,128)} %get-tuple-element.12.w_new, f32[4,96,256]{2,1,0:T(8,128)} %get-tuple-element.13.m_new, f32[60,96,256]{2,1,0:T(8,128)} %copy.16.w_ref.w_any, ...), custom_call_target="tpu_custom_call", output_to_operand_aliasing={{0}: (3, {}), {1}: (4, {})} | custom-call | tf_op jit(solution)/shard_map/put_rows/pallas_call | solution.py:256
  68.3 0.0 copy-done.1
  68.3 0.6 copy.11
  68.9 1.4 %reshape.13 = bf16[4,96,1024]{2,1,0:T(8,128)(2,1)} reshape(bf16[4,96,4,2,128]{4,3,2,1,0:T(2,128)(2,1)S(1)} %copy.11) | data formatting | bytes 1572864 | tf_op jit(solution)/shard_map/reshape | solution.py:267
Async XLA Ops:
  0.6 6.1 %copy-start = (f32[60,96,256]{2,1,0:T(8,128)S(1)}, f32[60,96,256]{2,1,0:T(8,128)}, u32[]{:S(2)}) copy-start(f32[60,96,256]{2,1,0:T(8,128)} %param.10) | copy-start | bytes 17694724
  64.2 4.1 %copy-start.1 = (bf16[2,2,8,96,128]{4,3,2,1,0:T(8,128)(2,1)S(1)}, bf16[2,2,8,96,128]{4,3,2,1,0:T(8,128)(2,1)}, u32[]{:S(2)}) copy-start(bf16[2,2,8,96,128]{4,3,2,1,0:T(8,128)(2,1)} %get-tuple-element.16) | copy-start | bytes 2359300

commit v2 on v1

--- a/solution.py
+++ b/solution.py
@@ -13,19 +13,29 @@
 MESH = pl.DeviceIdType.MESH
 
 
-def gather_body(ids, w_ref, m_ref, w_out, m_out):
-    w_out[...] = w_ref[...]
-    m_out[...] = m_ref[...]
-
-
-def scatter_body(ids, w_new, m_new, w_any, m_any, w_out, m_out):
-    w_out[...] = w_new[...]
-    m_out[...] = m_new[...]
-
-
-def reduce_body(sizes, counts, hidden, grad, w_rows, m_rows, w_new, m_new, shadow,
-                h_in, g_in, h_t, part, r_core, s_core, rx1, sx1, rx2, ry1, sy1, ry2, s_last, r_last,
-                in_sem, core_sem, one_sem, two_sem, last_sem, ag_sem, fw_sem):
+def table_body(ids, w_new, m_new, w_in, m_in, w_out, m_out, w_stage, m_stage, sem):
+    reads = [
+        pltpu.make_async_copy(w_in, w_stage, sem.at[0]),
+        pltpu.make_async_copy(m_in, m_stage, sem.at[1]),
+    ]
+    writes = [
+        pltpu.make_async_copy(w_stage, w_out, sem.at[2]),
+        pltpu.make_async_copy(m_stage, m_out, sem.at[3]),
+    ]
+    for copy in reads:
+        copy.start()
+    for read, stage, rows, write in zip(reads, (w_stage, m_stage), (w_new, m_new), writes):
+        read.wait()
+        for e in range(rows.shape[0]):
+            stage[ids[e]] = rows[e]
+        write.start()
+    for copy in writes:
+        copy.wait()
+
+
+def reduce_body(sizes, counts, ids, hidden, grad, master, momentum, w_new, m_new, shadow_out,
+                shadow, w_stage, m_stage, h_in, g_in, h_t, part, r_core, s_core, rx1, sx1, rx2, ry1, sy1, ry2, s_last, r_last,
+                in_sem, table_sem, core_sem, one_sem, two_sem, last_sem, ag_sem, fw_sem):
     experts, cap, outer_row, outer_col, feat, width, halves, scale = sizes
     chunks = experts * halves
     row, col = lax.axis_index("row"), lax.axis_index("col")
@@ -52,6 +62,12 @@
         for copy in pair:
             copy.start()
         loads.append(pair)
+    reads = [
+        pltpu.make_async_copy(master, w_stage, table_sem.at[0]),
+        pltpu.make_async_copy(momentum, m_stage, table_sem.at[1]),
+    ]
+    for copy in reads:
+        copy.start()
 
     barrier = pltpu.get_barrier_semaphore()
     greeted = [where for name in ("core", "x", "y", "z") for _, where in spots(name)]
@@ -149,9 +165,9 @@
         for d in range(outer_row - 1):
             total = total + r_last[c, d].astype(f32)
         e, lanes = c // halves, slice(c % halves * width, (c % halves + 1) * width)
-        moved = momentum_decay * m_rows[e, :, lanes] + total * f32(scale)
+        moved = momentum_decay * m_stage[ids[e], :, lanes] + total * f32(scale)
         m_new[e, :, lanes] = moved
-        stepped = w_rows[e, :, lanes] - step_size * moved
+        stepped = w_stage[ids[e], :, lanes] - step_size * moved
         w_new[e, :, lanes] = stepped
         shadow[y, core, c] = stepped.astype(bf16)
         own = shadow.at[y, core, c]
@@ -176,12 +192,20 @@
     for stage, e in plan:
         if stage == "m":
             multiply(e)
+            if e == experts - 1:
+                for read in reads:
+                    read.wait()
             continue
         for h in range(halves):
             stages[stage](e * halves + h)
     for c in range(chunks):
         for copy in flight["fw", c]:
             copy.wait_recv()
+        e, h = c // halves, c % halves
+        for b in range(outer_col):
+            for t in range(2):
+                at = ((b * 2 + t) * halves + h) * width
+                shadow_out[e, :, at:at + width] = shadow[b, t, c]
     for copy in started:
         copy.wait_send()
 
@@ -198,30 +222,23 @@
     scale = (cap * n_row * n_col) ** (-0.5)
     pairs = (chunks + 1) // 2
 
-    row_of = pl.BlockSpec((1, feat, block), lambda i, ids: (ids[i], 0, 0))
-    row_at = pl.BlockSpec((1, feat, block), lambda i, ids: (i, 0, 0))
     rows_type = jax.ShapeDtypeStruct((experts, feat, block), f32)
-    w_rows, m_rows = pl.pallas_call(
-        gather_body,
-        grid_spec=pltpu.PrefetchScalarGridSpec(
-            num_scalar_prefetch=1, grid=(experts,), in_specs=[row_of, row_of], out_specs=[row_at, row_at]
-        ),
-        out_shape=[rows_type, rows_type],
-        name="pick_rows",
-    )(shadow_ids, master, momentum)
-
+    table_type = jax.ShapeDtypeStruct(master.shape, f32)
     sizes = (experts, cap, outer_row, outer_col, feat, width, halves, scale)
     tail = (feat, width)
     oc1, or1 = max(outer_col - 1, 1), max(outer_row - 1, 1)
     vmem = pl.BlockSpec(memory_space=pltpu.VMEM)
     anywhere = pl.BlockSpec(memory_space=pl.ANY)
     dma = pltpu.SemaphoreType.DMA
-    w_new, m_new, shadow = pl.pallas_call(
+    w_new, m_new, shadow_out = pl.pallas_call(
         functools.partial(reduce_body, sizes),
-        in_specs=[pl.BlockSpec(memory_space=pltpu.SMEM), anywhere, anywhere, vmem, vmem],
-        out_specs=[vmem, vmem, vmem],
-        out_shape=[rows_type, rows_type, jax.ShapeDtypeStruct((outer_col, 2, chunks) + tail, bf16)],
+        in_specs=[pl.BlockSpec(memory_space=pltpu.SMEM)] * 2 + [anywhere] * 4,
+        out_specs=[vmem] * 3,
+        out_shape=[rows_type] * 2 + [jax.ShapeDtypeStruct((experts, feat, out), bf16)],
         scratch_shapes=[
+            pltpu.VMEM((outer_col, 2, chunks) + tail, bf16),
+            pltpu.VMEM(master.shape, f32),
+            pltpu.VMEM(master.shape, f32),
             pltpu.VMEM((experts, cap, hid), bf16),
             pltpu.VMEM((experts, cap, out), bf16),
             pltpu.VMEM((hid, cap), bf16),
@@ -237,6 +254,7 @@
             pltpu.VMEM((chunks, outer_row) + tail, bf16),
             pltpu.VMEM((chunks, or1) + tail, bf16),
             dma((2, experts)),
+            dma((2,)),
             dma((chunks, 2)),
             dma((chunks, oc1, 2)),
             dma((chunks, oc1, 2)),
@@ -251,20 +269,16 @@
             flops=2 * experts * cap * hid * out, bytes_accessed=2 * experts * cap * (hid + out), transcendentals=0
         ),
         name="reduce_step",
-    )(counts, hidden, grad_out, w_rows, m_rows)
+    )(counts, shadow_ids, hidden, grad_out, master, momentum)
 
     master_out, momentum_out = pl.pallas_call(
-        scatter_body,
-        grid_spec=pltpu.PrefetchScalarGridSpec(
-            num_scalar_prefetch=1, grid=(experts,),
-            in_specs=[row_at, row_at, anywhere, anywhere], out_specs=[row_of, row_of],
-        ),
-        out_shape=[jax.ShapeDtypeStruct(master.shape, f32)] * 2,
-        input_output_aliases={3: 0, 4: 1},
+        table_body,
+        in_specs=[pl.BlockSpec(memory_space=pltpu.SMEM), vmem, vmem, anywhere, anywhere],
+        out_specs=[anywhere, anywhere],
+        out_shape=[table_type] * 2,
+        scratch_shapes=[pltpu.VMEM(master.shape, f32), pltpu.VMEM(master.shape, f32), dma((4,))],
         name="put_rows",
     )(shadow_ids, w_new, m_new, master, momentum)
-    shadow = shadow.reshape(n_col, experts, halves, feat, width)
-    shadow_out = shadow.transpose(1, 3, 0, 2, 4).reshape(experts, feat, out)
     return (master_out, momentum_out, shadow_out)
 
 

time: 70.7 us -> 62.1 us (0.88)
  local copies, waits for them, and re-layouts: 10.7 us -> 0.89 us
  Pallas kernels: 58.9 us -> 60.4 us
    unnamed x6 -> x3, local copies, waits for them, and re-layouts: 8.66 us -> 0.89 us
    pallas_call x2 -> x1, Pallas kernels: 8.05 us -> 9.94 us  [shards(): pl.pallas_call(table_body, in_specs=[pl.BlockSpec(memory_space=pltpu.SMEM...]
    reshape x1 -> x0, local copies, waits for them, and re-layouts: 1.44 us -> none  [shards(): shadow_out = shadow.transpose(1, 3, 0, 2, 4).reshape(experts, feat, out)]
where the time goes in v2:
time: 62.1 us; the launch traced here: 62 us
  Pallas kernels  60.4 us (97%)
  local copies, waits for them, and re-layouts  0.89 us (1%)
  between operations  0.66 us (1%)
    pallas_call x1, Pallas kernels, shards(): pl.pallas_call(functools.partial(reduce_body, sizes), in_specs=[pl.BlockS...  50.5 us
    pallas_call x1, Pallas kernels, shards(): pl.pallas_call(table_body, in_specs=[pl.BlockSpec(memory_space=pltpu.SMEM...  9.94 us

profile of v2, /device:TPU:0, one launch (start us, length us, event | category | flops | bytes accessed | tf_op | source)
XLA Modules:
  0.0 62.0 jit_solution(12129092908834852418)
XLA Ops:
  0.6 50.5 %reduce_step.1 = (f32[4,96,256]{2,1,0:T(8,128)}, f32[4,96,256]{2,1,0:T(8,128)}, bf16[4,96,1024]{2,1,0:T(8,128)(2,1)}) custom-call(s32[1,4]{1,0:T(1,128)} %counts.1, s32[4]{0:T(128)} %ids.3, bf16[4,640,768]{2,1,0:T(8,128)(2,1)} %hidden.1, bf16[4,640,1024]{2,1,0:T(8,128)(2,1)} %grad.1, f32[60,96,256]{2,1,0:T(8,128)} %w_in.1, f32[60,96,256]{2,1,0:T(8,128)} %m_in.1), custom_call_target="tpu_custom_call" | custom-call | flops 4026531840 | bytes 9175040 | tf_op jit(solution)/shard_map/reduce_step/pallas_call | solution.py:233
  51.1 0.0 copy-start
  51.1 9.9 %put_rows.1 = (f32[60,96,256]{2,1,0:T(8,128)}, f32[60,96,256]{2,1,0:T(8,128)}) custom-call(s32[4]{0:T(128)} %ids.3, f32[4,96,256]{2,1,0:T(8,128)} %get-tuple-element.8.w_new, f32[4,96,256]{2,1,0:T(8,128)} %get-tuple-element.9.m_new, f32[60,96,256]{2,1,0:T(8,128)} %w_in.1, f32[60,96,256]{2,1,0:T(8,128)} %m_in.1), custom_call_target="tpu_custom_call" | custom-call | tf_op jit(solution)/shard_map/put_rows/pallas_call | solution.py:274
  61.1 0.0 copy-done
  61.1 0.9 %copy.10 = bf16[4,96,1024]{2,1,0:T(8,128)(2,1)} copy(bf16[4,96,1024]{2,1,0:T(8,128)(2,1)S(1)} %copy-done) | data formatting | bytes 1572864
Async XLA Ops:
  51.1 10.0 %copy-start = (bf16[4,96,1024]{2,1,0:T(8,128)(2,1)S(1)}, bf16[4,96,1024]{2,1,0:T(8,128)(2,1)}, u32[]{:S(2)}) copy-start(bf16[4,96,1024]{2,1,0:T(8,128)(2,1)} %get-tuple-element.18) | copy-start | bytes 2359300
